TPU v7x, 32 devices: a whole 2x2x4 slice. The times are simulated.
32 devices in a mesh: section: 2 (over x), expert: 16 (over z, y, core).
Axes of the slice: x: 2, y: 2, z: 4, core: 2. Of those that a mesh axis runs over, the one named last changes fastest.
Arguments:
- images: bfloat16 [32, 256, 1408], P(('section', 'expert')), may hold values from -6 to 6
- norm_gain: bfloat16 [1408], replicated, may hold values from 0.5 to 1.5
- slot_map: bfloat16 [1408, 16], replicated, may hold values from -0.15625 to 0.15625
- logit_scale: float32 [1], replicated, may hold values from 30 to 80
- up_weight: bfloat16 [16, 5120, 1408], P('expert', 'section'), may hold values from -0.625 to 0.625
- down_weight: bfloat16 [16, 5120, 1408], P('expert', 'section'), may hold values from -0.3125 to 0.3125
Outputs:
- block_out: bfloat16 [32, 256, 1408], P(('section', 'expert'))
All inputs are finite; a program needn't handle non-finite values.
Results may differ from a plain program's by a relative error of at most 0.011.
Values may be sent and summed in bfloat16 or wider, within the bound.
A program may use at most 64 MiB of HBM per device.

v0:
```python
import jax
import jax.numpy as jnp
from jax import lax
from jax.sharding import PartitionSpec as P

epsilon = 1e-06


def normalize(inputs, gain_row):
    values = inputs.astype(jnp.float32)
    spread = jnp.mean(values * values, axis=-1, keepdims=True)
    return (values * lax.rsqrt(spread + epsilon) * gain_row.astype(jnp.float32)).astype(
        jnp.bfloat16
    )


def weights_from(raw, normed, slot_cols, scale_now):
    values = normed.astype(jnp.float32)
    token_norm = jnp.sqrt(jnp.sum(values * values, axis=-1) + epsilon)
    columns = slot_cols.astype(jnp.float32)
    column_norm = jnp.sqrt(jnp.sum(columns * columns, axis=0) + epsilon)
    logits = scale_now * raw / (token_norm[:, None, :] * column_norm[None, :, None])
    scores = jnp.exp(logits)
    dispatch = (scores / jnp.sum(scores, axis=-1, keepdims=True)).astype(jnp.bfloat16)
    combine = (scores / jnp.sum(scores, axis=1, keepdims=True)).astype(jnp.bfloat16)
    return (dispatch, combine)


def local(images, norm_gain, slot_map, logit_scale, up_weight, down_weight):
    position = lax.axis_index("section")
    normed = normalize(images, norm_gain)
    raw = jnp.einsum("itd,de->iet", normed, slot_map, preferred_element_type=jnp.float32)
    dispatch, combine = weights_from(raw, normed, slot_map, logit_scale[0])
    slot_in = jnp.einsum(
        "iet,itd->eid", dispatch, normed, preferred_element_type=jnp.float32
    ).astype(jnp.bfloat16)
    slots = lax.all_to_all(slot_in, "expert", split_axis=0, concat_axis=1, tiled=True)
    count = slots.shape[1]
    gathered = lax.all_gather(slots, "section", axis=1, tiled=True)
    hidden = jax.nn.gelu(
        jnp.einsum("esd,efd->esf", gathered, up_weight, preferred_element_type=jnp.float32)
    ).astype(jnp.bfloat16)
    partial_sum = jnp.einsum(
        "esf,efd->esd", hidden, down_weight, preferred_element_type=jnp.float32
    )
    totals = lax.psum(partial_sum, "section")
    own_rows = lax.dynamic_slice_in_dim(totals, position * count, count, 1)
    result = own_rows.astype(jnp.bfloat16)
    back = lax.all_to_all(result, "expert", split_axis=1, concat_axis=0, tiled=True)
    mixed = jnp.einsum("iet,eid->itd", combine, back, preferred_element_type=jnp.float32)
    return (images.astype(jnp.float32) + mixed).astype(jnp.bfloat16)


def solution(mesh):
    return jax.shard_map(
        local,
        mesh=mesh,
        in_specs=(
            P(("section", "expert"), None, None),
            P(),
            P(),
            P(),
            P("expert", "section", None),
            P("expert", "section", None),
        ),
        out_specs=P(("section", "expert"), None, None),
        check_vma=False,
    )
```

profile of v0, /device:TPU:0, one launch (start us, length us, event | category | flops | bytes accessed | tf_op | source)
XLA Modules:
  0.0 58.3 jit_solution(4352403339752684257)
XLA Ops:
  0.0 0.0 copy-start.1
  0.0 0.0 copy-start
  0.7 0.9 %multiply_reduce_fusion.1 = f32[16]{0:T(128)S(1)} fusion(bf16[1408,16]{0,1:T(8,128)(2,1)} %param.8), kind=kLoop, calls=%fused_computation.37 | loop fusion | flops 67568 | bytes 45120 | tf_op jit(solution)/shard_map/reduce_sum | solution.py:21
  1.6 1.3 %fusion.10 = f32[256]{0:T(256)S(1)} fusion(bf16[1,256,1408]{2,1,0:T(8,128)(2,1)} %param.6), kind=kLoop, calls=%fused_computation.12 | loop fusion | flops 1081088 | bytes 721920 | tf_op jit(solution)/shard_map/reduce_sum | solution.py:11
  3.0 0.7 %convert_element_type.44 = f32[1408]{0:T(1024)S(1)} convert(bf16[1408]{0:T(1024)(128)(2,1)} %param.7) | non-fusion elementwise | flops 1408 | bytes 8448 | tf_op jit(solution)/shard_map/convert_element_type | solution.py:12
  3.7 1.5 %multiply_reduce_fusion = f32[256]{0:T(256)S(1)} fusion(f32[1408]{0:T(1024)S(1)} %convert_element_type.44, f32[256]{0:T(256)S(1)} %add_rsqrt_fusion, bf16[1,256,1408]{2,1,0:T(8,128)(2,1)} %param.6), kind=kLoop, calls=%fused_computation.15 | loop fusion | flops 2522880 | bytes 728576 | tf_op jit(solution)/shard_map/reduce_sum | solution.py:19
  5.2 0.0 copy-done.1
  5.2 0.0 copy-done
  5.2 0.5 fusion.48
  5.7 0.4 fusion.9
  6.1 0.6 %broadcast.46 = bf16[]{:T(256)} broadcast(bf16[]{:T(256)} %constant.65), dimensions={} | broadcast | bytes 4 | tf_op jit(solution)/shard_map/convert_element_type | solution.py:36
  6.7 0.7 %reduce.6 = bf16[16,1408]{1,0:T(8,128)(2,1)S(1)} reduce(bf16[16,1,1408]{2,0,1:T(8,128)(2,1)S(1)} %fusion.9, bf16[]{:T(256)} %broadcast.46), dimensions={1}, to_apply=%copy.9.reduce_sub_computation | reduce | bytes 90114 | tf_op jit(solution)/shard_map/convert_element_type | solution.py:36
  7.4 0.7 %reshape.104 = bf16[16,2,704]{2,1,0:T(2,128)(2,1)} reshape(bf16[16,1408]{1,0:T(8,128)(2,1)S(1)} %reduce.6) | data formatting | bytes 90112
  8.1 7.4 %all-to-all-start = ((bf16[16,2,704]{2,1,0:T(2,128)(2,1)}), bf16[16,2,704]{2,1,0:T(2,128)(2,1)S(1)}, u32[]{:S(2)}, u32[]{:S(2)}) async-start(bf16[16,2,704]{2,1,0:T(2,128)(2,1)} %reshape.104), calls=%async_computation | async-start | bytes 98304 | tf_op jit(solution)/shard_map/all_to_all | solution.py:37
  15.5 6.8 %all-to-all-done = bf16[16,2,704]{2,1,0:T(2,128)(2,1)S(1)} async-done(((bf16[16,2,704]{2,1,0:T(2,128)(2,1)}), bf16[16,2,704]{2,1,0:T(2,128)(2,1)S(1)}, u32[]{:S(2)}, u32[]{:S(2)}) %all-to-all-start) | async-done | bytes 45088 | tf_op jit(solution)/shard_map/all_to_all | solution.py:37
  22.3 0.1 reshape.105
  22.4 4.7 %all-gather = bf16[32,1,1408]{2,0,1:T(8,128)(2,1)S(1)} all-gather(bf16[16,1,1408]{2,0,1:T(8,128)(2,1)S(1)} %copy.10), channel_id=2, replica_groups=mesh['section'=2,'expert'=16] {'section'}, dimensions={0}, use_global_device_ids=true | all-gather | bytes 135168 | tf_op jit(solution)/shard_map/all_gather | solution.py:39
  27.2 8.4 %fusion.6 = f32[1,32,1408]{2,1,0:T(8,128)S(1)} fusion(bf16[1,2560,1408]{2,1,0:T(8,128)(2,1)} %param.11, bf16[1,2560,1408]{2,1,0:T(8,128)(2,1)} %param.10, bf16[32,1,1408]{2,0,1:T(8,128)(2,1)S(1)} %all-gather), kind=kOutput, calls=%fused_computation.7 | convolution fusion | flops 462110720 | bytes 14688256 | tf_op jit(solution)/shard_map/esf,efd->esd/dot_general | solution.py:43
  35.6 10.9 %all-reduce.1 = bf16[1,32,1408]{2,1,0:T(8,128)(2,1)S(1)} all-reduce(f32[1,32,1408]{2,1,0:T(8,128)S(1)} %fusion.6), channel_id=1, replica_groups=mesh['section'=2,'expert'=16] {'section'}, use_global_device_ids=true, to_apply=%region_5.0 | all-reduce | flops 45056 | bytes 270336 | tf_op jit(solution)/shard_map/psum | solution.py:46
  46.5 0.1 copy.18
  46.6 0.9 %reduce.7 = bf16[16,1408]{1,0:T(8,128)(2,1)S(1)} reduce(bf16[16,1,1408]{2,1,0:T(2,128)(2,1)S(1)} %bitcast.53, bf16[]{:T(256)} %broadcast.46), dimensions={1}, to_apply=%bitcast.51.reduce_sub_computation | reduce | bytes 90114
  47.5 0.1 reshape.106
  47.6 9.3 %all_to_all.21 = bf16[16,2,704]{2,1,0:T(2,128)(2,1)S(1)} all-to-all(bf16[16,2,704]{2,1,0:T(2,128)(2,1)S(1)} %reshape.106), channel_id=1, replica_groups=mesh['section'=2,'expert'=16] {'expert'}, dimensions={0} | all-to-all | bytes 90112 | tf_op jit(solution)/shard_map/all_to_all | solution.py:49
  57.0 0.1 reshape.107
  57.1 1.3 %fusion.5 = bf16[1,256,1408]{2,1,0:T(8,128)(2,1)} fusion(bf16[1,256,1408]{2,1,0:T(8,128)(2,1)S(1)} %copy-done, bf16[1,16,1408]{2,0,1:T(2,128)(2,1)S(1)} %bitcast.54, f32[16,256]{1,0:T(8,128)S(1)} %get-tuple-element.7, f32[256]{0:T(256)S(1)} %get-tuple-element.5), kind=kOutput, calls=%fused_computation.6 | convolution fusion | flops 12623872 | bytes 1504256 | tf_op jit(solution)/shard_map/iet,eid->itd/dot_general | solution.py:50
  (5 shorter events, 0.1 us)
Async XLA Ops:
  0.0 5.2 %copy-start.1 = (bf16[1408,16]{0,1:T(8,128)(2,1)S(1)}, bf16[1408,16]{0,1:T(8,128)(2,1)}, u32[]{:S(2)}) copy-start(bf16[1408,16]{0,1:T(8,128)(2,1)} %param.8) | copy-start | bytes 135172
  0.0 5.2 %copy-start = (bf16[1,256,1408]{2,1,0:T(8,128)(2,1)S(1)}, bf16[1,256,1408]{2,1,0:T(8,128)(2,1)}, u32[]{:S(2)}) copy-start(bf16[1,256,1408]{2,1,0:T(8,128)(2,1)} %param.6) | copy-start | bytes 2162692
  8.1 14.2 %all-to-all-start = ((bf16[16,2,704]{2,1,0:T(2,128)(2,1)}), bf16[16,2,704]{2,1,0:T(2,128)(2,1)S(1)}, u32[]{:S(2)}, u32[]{:S(2)}) async-start(bf16[16,2,704]{2,1,0:T(2,128)(2,1)} %reshape.104), calls=%async_computation | async-start | bytes 98304 | tf_op jit(solution)/shard_map/all_to_all | solution.py:37
where the time goes:
time: 58.8 us; the launch traced here: 58.3 us
  blocking collectives  24.9 us (42%)
  matrix products  10.6 us (18%)
  starting transfers between devices  7.41 us (13%)
  waiting for transfers between devices  6.76 us (11%)
  other arithmetic  6.08 us (10%)
  local copies, waits for them, and re-layouts  1.79 us (3%)
  between operations  0.82 us (1%)
    psum x1, blocking collectives, local(): totals = lax.psum(partial_sum, 'section')  10.9 us
    all_to_all x1, blocking collectives, local(): lax.all_to_all(result, 'expert', split_axis=1, concat_axis=0, tiled=True)  9.34 us
    dot_general x1, matrix products, local(): jnp.einsum('esf,efd->esd', hidden, down_weight, preferred_element_type=jn...  8.44 us
    all_to_all x1, starting transfers between devices, local(): lax.all_to_all(slot_in, 'expert', split_axis=0, concat_axis=1, tiled=True)  7.41 us
    all_to_all x1, waiting for transfers between devices, local(): lax.all_to_all(slot_in, 'expert', split_axis=0, concat_axis=1, tiled=True)  6.76 us
    all_gather x1, blocking collectives, local(): gathered = lax.all_gather(slots, 'section', axis=1, tiled=True)  4.71 us
    reduce_sum x1, other arithmetic, weights_from(): token_norm = jnp.sqrt(jnp.sum(values * values, axis=-1) + epsilon)  1.48 us
    reduce_sum x1, other arithmetic, normalize(): spread = jnp.mean(values * values, axis=-1, keepdims=True)  1.34 us
  transfers between devices with their start and end apart: 1, of which 1 were waited for; matrix products, arithmetic and copies ran while one was open for 0% of the time, Pallas kernels for 0%

commit v1 on v0

v1 whole, which is shorter than its diff:
```python
import functools

import jax
import jax.numpy as jnp
from jax import lax
from jax.experimental import pallas as pl
from jax.experimental.pallas import tpu as pltpu
from jax.sharding import PartitionSpec as P

epsilon = 1e-06
MESH = pl.DeviceIdType.MESH
NT = (((1,), (1,)), ((), ()))
TN = (((0,), (0,)), ((), ()))


def split_of(total, most, unit):
    best = unit
    for size in range(unit, most + 1, unit):
        if total % size == 0:
            best = size
    return best


def kernel(
    sections, experts, chunk,
    x_hbm, gain_ref, slot_ref, scale_ref, up_hbm, down_hbm,
    out_hbm,
    xs, normed, stat, up_v, down_v, send1, recv1, send2, recv2, out_v,
    x_sem, up_sem, down_sem, out_sem, local_sem, send_sem, recv_sem,
):
    n = sections * experts
    tokens, width = xs.shape
    half = send1.shape[2]
    rest = width - half
    hidden_units = up_v.shape[0]
    chunks = hidden_units // chunk
    section = lax.axis_index("section")
    expert = lax.axis_index("expert")
    me = section * experts + expert

    x_parts = x_sem.shape[0]
    x_rows = tokens // x_parts
    x_copies = [
        pltpu.make_async_copy(
            x_hbm.at[pl.ds(i * x_rows, x_rows)], xs.at[pl.ds(i * x_rows, x_rows)], x_sem.at[i]
        )
        for i in range(x_parts)
    ]
    for copy in x_copies:
        copy.start()

    barrier = pltpu.get_barrier_semaphore()

    def coords(k):
        target = lax.rem(me + k, n)
        return target, lax.div(target, experts), lax.rem(target, experts)

    def greet(k, carry):
        _, s, e = coords(k)
        pl.semaphore_signal(barrier, inc=1, device_id={"section": s, "expert": e}, device_id_type=MESH)
        return carry

    lax.fori_loop(1, n, greet, 0)

    up_copies = []
    down_copies = []
    for c in range(chunks):
        rows = pl.ds(c * chunk, chunk)
        up_copies.append(pltpu.make_async_copy(up_hbm.at[rows], up_v.at[rows], up_sem.at[c]))
        down_copies.append(pltpu.make_async_copy(down_hbm.at[rows], down_v.at[rows], down_sem.at[c]))
    for copy in up_copies + down_copies:
        copy.start()

    columns = slot_ref[...].astype(jnp.float32)
    column_norm = jnp.sqrt(jnp.sum(columns * columns, axis=-1, keepdims=True) + epsilon)
    gain = gain_ref[...].astype(jnp.float32)

    step_rows = 16

    def norm_step(i, carry):
        rows = pl.ds(pl.multiple_of(i * step_rows, step_rows), step_rows)
        values = xs[rows, :].astype(jnp.float32)
        spread = jnp.sum(values * values, axis=-1, keepdims=True) * (1.0 / width)
        result = (values * lax.rsqrt(spread + epsilon) * gain).astype(jnp.bfloat16)
        normed[rows, :] = result
        wide = result.astype(jnp.float32)
        square = jnp.sum(wide * wide, axis=-1, keepdims=True)
        stat[rows, :] = jnp.broadcast_to(square, (step_rows, stat.shape[1]))
        return carry

    per = x_rows // step_rows
    for i, copy in enumerate(x_copies):
        copy.wait()
        lax.fori_loop(i * per, (i + 1) * per, norm_step, 0, unroll=True)

    raw = lax.dot_general(slot_ref[...], normed[...], NT, preferred_element_type=jnp.float32)
    token_norm = jnp.sqrt(jnp.transpose(stat[...])[0:1, :] + epsilon)
    logits = scale_ref[0] * raw / (token_norm * column_norm)
    scores = jnp.exp(logits)
    dispatch = (scores / jnp.sum(scores, axis=1, keepdims=True)).astype(jnp.bfloat16)
    combine = (scores / jnp.sum(scores, axis=0, keepdims=True)).astype(jnp.bfloat16)
    slot_in = jnp.dot(dispatch, normed[...], preferred_element_type=jnp.float32).astype(jnp.bfloat16)
    send1[:, 0, :] = slot_in[:, :half]
    send1[:, 1, :rest] = slot_in[:, half:]

    pl.semaphore_wait(barrier, n - 1)

    own1 = pltpu.make_async_copy(send1.at[expert], recv1.at[me], local_sem.at[0])
    own1.start()

    def dispatch_row(k, carry):
        _, s, e = coords(k)
        pltpu.make_async_remote_copy(
            src_ref=send1.at[e], dst_ref=recv1.at[me], send_sem=send_sem.at[0], recv_sem=recv_sem.at[0],
            device_id={"section": s, "expert": e}, device_id_type=MESH,
        ).start()
        return carry

    lax.fori_loop(1, n, dispatch_row, 0)

    def wait_all(buffer, sem):
        part = buffer.at[pl.ds(0, n - 1)]
        pltpu.make_async_copy(part, part, sem).wait()

    own1.wait()
    wait_all(recv1, recv_sem.at[0])
    left = recv1[:, 0, :]
    right = recv1[:, 1, :rest]
    rows_in = jnp.concatenate([left, right], axis=1)
    total = None
    for c in range(chunks):
        rows = pl.ds(c * chunk, chunk)
        up_copies[c].wait()
        pre = lax.dot_general(rows_in, up_v[rows, :], NT, preferred_element_type=jnp.float32)
        act = jax.nn.gelu(pre).astype(jnp.bfloat16)
        down_copies[c].wait()
        term = jnp.dot(act, down_v[rows, :], preferred_element_type=jnp.float32)
        total = term if total is None else total + term
    partial = total.astype(jnp.bfloat16)
    send2[:, 0, :] = partial[:, :half]
    send2[:, 1, :rest] = partial[:, half:]

    own2 = pltpu.make_async_copy(send2.at[me], recv2.at[me], local_sem.at[1])
    own2.start()

    def return_row(k, carry):
        target, s, e = coords(k)
        pltpu.make_async_remote_copy(
            src_ref=send2.at[target], dst_ref=recv2.at[me], send_sem=send_sem.at[1], recv_sem=recv_sem.at[1],
            device_id={"section": s, "expert": e}, device_id_type=MESH,
        ).start()
        return carry

    lax.fori_loop(1, n, return_row, 0)

    own2.wait()
    wait_all(recv2, recv_sem.at[1])
    summed = recv2[pl.ds(0, experts)].astype(jnp.float32)
    for s in range(1, sections):
        summed = summed + recv2[pl.ds(s * experts, experts)].astype(jnp.float32)
    slot_out = summed.astype(jnp.bfloat16)
    slot_out = jnp.concatenate([slot_out[:, 0, :], slot_out[:, 1, :rest]], axis=1)

    o_parts = out_sem.shape[0]
    o_rows = tokens // o_parts
    copies = []
    for i in range(o_parts):
        rows = pl.ds(i * o_rows, o_rows)
        mixed = lax.dot_general(
            combine[:, i * o_rows:(i + 1) * o_rows], slot_out, TN, preferred_element_type=jnp.float32
        )
        out_v[rows, :] = (xs[rows, :].astype(jnp.float32) + mixed).astype(jnp.bfloat16)
        copy = pltpu.make_async_copy(out_v.at[rows], out_hbm.at[rows], out_sem.at[i])
        copy.start()
        copies.append(copy)
    wait_all(recv1, send_sem.at[0])
    wait_all(recv2, send_sem.at[1])
    for copy in copies:
        copy.wait()


def solution(mesh):
    sections, experts = mesh.shape["section"], mesh.shape["expert"]
    n = sections * experts

    def local(images, norm_gain, slot_map, logit_scale, up_weight, down_weight):
        count, tokens, width = images.shape
        held, hidden_units, _ = up_weight.shape
        slots = slot_map.shape[1]
        assert count == 1 and held == 1 and slots == experts
        half = -(-width // 256) * 128
        chunk = split_of(hidden_units, 512, 128)
        chunks = hidden_units // chunk
        bf16 = jnp.bfloat16
        hbm = pl.BlockSpec(memory_space=pl.ANY)
        vmem = pl.BlockSpec(memory_space=pltpu.VMEM)
        x_parts, o_parts = 4, 2
        result = pl.pallas_call(
            functools.partial(kernel, sections, experts, chunk),
            out_shape=jax.ShapeDtypeStruct((tokens, width), bf16),
            in_specs=[hbm, vmem, vmem, pl.BlockSpec(memory_space=pltpu.SMEM), hbm, hbm],
            out_specs=hbm,
            scratch_shapes=[
                pltpu.VMEM((tokens, width), bf16),
                pltpu.VMEM((tokens, width), bf16),
                pltpu.VMEM((tokens, 128), jnp.float32),
                pltpu.VMEM((hidden_units, width), bf16),
                pltpu.VMEM((hidden_units, width), bf16),
                pltpu.VMEM((experts, 2, half), bf16),
                pltpu.VMEM((n, 2, half), bf16),
                pltpu.VMEM((n, 2, half), bf16),
                pltpu.VMEM((n, 2, half), bf16),
                pltpu.VMEM((tokens, width), bf16),
                pltpu.SemaphoreType.DMA((x_parts,)),
                pltpu.SemaphoreType.DMA((chunks,)),
                pltpu.SemaphoreType.DMA((chunks,)),
                pltpu.SemaphoreType.DMA((o_parts,)),
                pltpu.SemaphoreType.DMA((2,)),
                pltpu.SemaphoreType.DMA((2,)),
                pltpu.SemaphoreType.DMA((2,)),
            ],
            compiler_params=pltpu.CompilerParams(
                collective_id=0, has_side_effects=True, vmem_limit_bytes=60 * 1024 * 1024
            ),
        )(
            images.reshape(tokens, width), norm_gain.reshape(1, width), slot_map.T, logit_scale,
            up_weight.reshape(hidden_units, width), down_weight.reshape(hidden_units, width),
        )
        return result.reshape(1, tokens, width)

    return jax.shard_map(
        local,
        mesh=mesh,
        in_specs=(
            P(("section", "expert"), None, None),
            P(),
            P(),
            P(),
            P("expert", "section", None),
            P("expert", "section", None),
        ),
        out_specs=P(("section", "expert"), None, None),
        check_vma=False,
    )
```

time: 58.8 us -> 28.1 us (0.48)
  blocking collectives: 24.9 us -> 0 us
  Pallas kernels: 0 us -> 23.9 us
  matrix products: 10.6 us -> 0 us
  starting transfers between devices: 7.41 us -> 0 us
  waiting for transfers between devices: 6.76 us -> 0 us
  other arithmetic: 6.08 us -> 0 us
  local copies, waits for them, and re-layouts: 1.79 us -> 3.31 us
    pallas_call x0 -> x1, Pallas kernels: none -> 23.9 us  [local(): pl.pallas_call(functools.partial(kernel, sections, experts, chunk), out_s...]
    psum x1 -> x0, blocking collectives: 10.9 us -> none  [local(): totals = lax.psum(partial_sum, 'section')]
    dot_general x4 -> x0, matrix products: 10.6 us -> none  [the longest x1 8.44 us: local(): jnp.einsum('esf,efd->esd', hidden, down_weight, preferred_element_type=jn...]
    all_to_all x1 -> x0, blocking collectives: 9.34 us -> none  [local(): lax.all_to_all(result, 'expert', split_axis=1, concat_axis=0, tiled=True)]
    all_to_all x1 -> x0, starting transfers between devices: 7.41 us -> none  [local(): lax.all_to_all(slot_in, 'expert', split_axis=0, concat_axis=1, tiled=True)]
    all_to_all x1 -> x0, waiting for transfers between devices: 6.76 us -> none  [local(): lax.all_to_all(slot_in, 'expert', split_axis=0, concat_axis=1, tiled=True)]
    all_gather x1 -> x0, blocking collectives: 4.71 us -> none  [local(): gathered = lax.all_gather(slots, 'section', axis=1, tiled=True)]
    reduce_sum x3 -> x0, other arithmetic: 3.73 us -> none  [the longest x1 1.48 us: weights_from(): token_norm = jnp.sqrt(jnp.sum(values * values, axis=-1) + epsilon)]
  transfers between devices with their start and end apart: 1 -> 0, of which waited for: 1 -> 0; matrix products, arithmetic and copies ran while one was open for 0% -> 0% of each run, Pallas kernels for 0% -> 0%
where the time goes in v1:
time: 28.1 us; the launch traced here: 27.9 us
  Pallas kernels  23.9 us (85%)
  local copies, waits for them, and re-layouts  3.31 us (12%)
  between operations  0.66 us (2%)
    pallas_call x1, Pallas kernels, local(): pl.pallas_call(functools.partial(kernel, sections, experts, chunk), out_s...  23.9 us
    unnamed x1, local copies, waits for them, and re-layouts  2.02 us
    reshape x1, local copies, waits for them, and re-layouts, local(): norm_gain.reshape(1, width)  1.28 us

profile of v1, /device:TPU:0, one launch (start us, length us, event | category | flops | bytes accessed | tf_op | source)
XLA Modules:
  0.0 27.9 jit_solution(8839326029823112687)
XLA Ops:
  0.7 1.3 %reshape.16.gain_ref = bf16[1,1408]{1,0:T(2,128)(2,1)} reshape(bf16[1408]{0:T(1024)(128)(2,1)} %param.7) | data formatting | bytes 5632 | tf_op jit(solution)/shard_map/reshape | solution.py:226
  1.9 23.9 %shard_map.64 = bf16[256,1408]{1,0:T(8,128)(2,1)} custom-call(bf16[256,1408]{1,0:T(8,128)(2,1)} %bitcast.8, bf16[1,1408]{1,0:T(2,128)(2,1)} %reshape.16.gain_ref, bf16[16,1408]{1,0:T(8,128)(2,1)} %bitcast.9, f32[1]{0:T(128)S(6)} %copy.8.scale_ref, bf16[2560,1408]{1,0:T(8,128)(2,1)} %bitcast.5, bf16[2560,1408]{1,0:T(8,128)(2,1)} %bitcast.6), custom_call_target="tpu_custom_call" | custom-call | tf_op jit(solution)/shard_map/pallas_call | solution.py:198
  25.8 2.0 %copy.9 = bf16[1,256,1408]{2,1,0:T(8,128)(2,1)} copy(bf16[1,256,1408]{2,1,0:T(8,128)(2,1)} %bitcast.7) | data formatting | bytes 1441792

commit v2 on v1

--- a/solution.py
+++ b/solution.py
@@ -24,9 +24,9 @@
 def kernel(
     sections, experts, chunk,
     x_hbm, gain_ref, slot_ref, scale_ref, up_hbm, down_hbm,
-    out_hbm,
-    xs, normed, stat, up_v, down_v, send1, recv1, send2, recv2, out_v,
-    x_sem, up_sem, down_sem, out_sem, local_sem, send_sem, recv_sem,
+    out_v,
+    xs, normed, stat, up_v, down_v, send1, recv1, send2, recv2,
+    x_sem, up_sem, down_sem, local_sem, send_sem, recv_sem,
 ):
     n = sections * experts
     tokens, width = xs.shape
@@ -51,16 +51,26 @@
 
     barrier = pltpu.get_barrier_semaphore()
 
-    def coords(k):
-        target = lax.rem(me + k, n)
-        return target, lax.div(target, experts), lax.rem(target, experts)
-
-    def greet(k, carry):
-        _, s, e = coords(k)
-        pl.semaphore_signal(barrier, inc=1, device_id={"section": s, "expert": e}, device_id_type=MESH)
-        return carry
-
-    lax.fori_loop(1, n, greet, 0)
+    def wrapped(value, bound):
+        return jnp.where(value >= bound, value - bound, value)
+
+    def for_others(visit):
+        def step(k, carry):
+            s = wrapped(section + k // experts, sections)
+            e = wrapped(expert + k % experts, experts)
+            visit(s * experts + e, e, {"section": s, "expert": e})
+            return carry
+
+        if n <= 64:
+            for k in range(n - 1, 0, -1):
+                step(k, 0)
+        else:
+            lax.fori_loop(1, n, step, 0)
+
+    def greet(target, e, device):
+        pl.semaphore_signal(barrier, inc=1, device_id=device, device_id_type=MESH)
+
+    for_others(greet)
 
     up_copies = []
     down_copies = []
@@ -73,7 +83,7 @@
 
     columns = slot_ref[...].astype(jnp.float32)
     column_norm = jnp.sqrt(jnp.sum(columns * columns, axis=-1, keepdims=True) + epsilon)
-    gain = gain_ref[...].astype(jnp.float32)
+    gain = gain_ref[...].astype(jnp.float32).reshape(1, width)
 
     step_rows = 16
 
@@ -108,15 +118,13 @@
     own1 = pltpu.make_async_copy(send1.at[expert], recv1.at[me], local_sem.at[0])
     own1.start()
 
-    def dispatch_row(k, carry):
-        _, s, e = coords(k)
+    def dispatch_row(target, e, device):
         pltpu.make_async_remote_copy(
             src_ref=send1.at[e], dst_ref=recv1.at[me], send_sem=send_sem.at[0], recv_sem=recv_sem.at[0],
-            device_id={"section": s, "expert": e}, device_id_type=MESH,
+            device_id=device, device_id_type=MESH,
         ).start()
-        return carry
-
-    lax.fori_loop(1, n, dispatch_row, 0)
+
+    for_others(dispatch_row)
 
     def wait_all(buffer, sem):
         part = buffer.at[pl.ds(0, n - 1)]
@@ -143,15 +151,13 @@
     own2 = pltpu.make_async_copy(send2.at[me], recv2.at[me], local_sem.at[1])
     own2.start()
 
-    def return_row(k, carry):
-        target, s, e = coords(k)
+    def return_row(target, e, device):
         pltpu.make_async_remote_copy(
             src_ref=send2.at[target], dst_ref=recv2.at[me], send_sem=send_sem.at[1], recv_sem=recv_sem.at[1],
-            device_id={"section": s, "expert": e}, device_id_type=MESH,
+            device_id=device, device_id_type=MESH,
         ).start()
-        return carry
-
-    lax.fori_loop(1, n, return_row, 0)
+
+    for_others(return_row)
 
     own2.wait()
     wait_all(recv2, recv_sem.at[1])
@@ -161,22 +167,16 @@
     slot_out = summed.astype(jnp.bfloat16)
     slot_out = jnp.concatenate([slot_out[:, 0, :], slot_out[:, 1, :rest]], axis=1)
 
-    o_parts = out_sem.shape[0]
+    o_parts = 4
     o_rows = tokens // o_parts
-    copies = []
     for i in range(o_parts):
         rows = pl.ds(i * o_rows, o_rows)
         mixed = lax.dot_general(
             combine[:, i * o_rows:(i + 1) * o_rows], slot_out, TN, preferred_element_type=jnp.float32
         )
         out_v[rows, :] = (xs[rows, :].astype(jnp.float32) + mixed).astype(jnp.bfloat16)
-        copy = pltpu.make_async_copy(out_v.at[rows], out_hbm.at[rows], out_sem.at[i])
-        copy.start()
-        copies.append(copy)
     wait_all(recv1, send_sem.at[0])
     wait_all(recv2, send_sem.at[1])
-    for copy in copies:
-        copy.wait()
 
 
 def solution(mesh):
@@ -194,12 +194,12 @@
         bf16 = jnp.bfloat16
         hbm = pl.BlockSpec(memory_space=pl.ANY)
         vmem = pl.BlockSpec(memory_space=pltpu.VMEM)
-        x_parts, o_parts = 4, 2
+        x_parts = 4
         result = pl.pallas_call(
             functools.partial(kernel, sections, experts, chunk),
-            out_shape=jax.ShapeDtypeStruct((tokens, width), bf16),
+            out_shape=pltpu.VMEM((tokens, width), bf16),
             in_specs=[hbm, vmem, vmem, pl.BlockSpec(memory_space=pltpu.SMEM), hbm, hbm],
-            out_specs=hbm,
+            out_specs=vmem,
             scratch_shapes=[
                 pltpu.VMEM((tokens, width), bf16),
                 pltpu.VMEM((tokens, width), bf16),
@@ -210,11 +210,9 @@
                 pltpu.VMEM((n, 2, half), bf16),
                 pltpu.VMEM((n, 2, half), bf16),
                 pltpu.VMEM((n, 2, half), bf16),
-                pltpu.VMEM((tokens, width), bf16),
                 pltpu.SemaphoreType.DMA((x_parts,)),
                 pltpu.SemaphoreType.DMA((chunks,)),
                 pltpu.SemaphoreType.DMA((chunks,)),
-                pltpu.SemaphoreType.DMA((o_parts,)),
                 pltpu.SemaphoreType.DMA((2,)),
                 pltpu.SemaphoreType.DMA((2,)),
                 pltpu.SemaphoreType.DMA((2,)),
@@ -223,7 +221,7 @@
                 collective_id=0, has_side_effects=True, vmem_limit_bytes=60 * 1024 * 1024
             ),
         )(
-            images.reshape(tokens, width), norm_gain.reshape(1, width), slot_map.T, logit_scale,
+            images.reshape(tokens, width), norm_gain, slot_map.T, logit_scale,
             up_weight.reshape(hidden_units, width), down_weight.reshape(hidden_units, width),
         )
         return result.reshape(1, tokens, width)

time: 28.1 us -> 24.5 us (0.87)
  local copies, waits for them, and re-layouts: 3.31 us -> 0.86 us
  Pallas kernels: 23.9 us -> 22.8 us
    reshape x1 -> x0, local copies, waits for them, and re-layouts: 1.28 us -> none  [local(): norm_gain.reshape(1, width)]
    unnamed x1, local copies, waits for them, and re-layouts: 2.02 us -> 0.86 us
    pallas_call x1, Pallas kernels: 23.9 us -> 22.8 us  [local(): pl.pallas_call(functools.partial(kernel, sections, experts, chunk), out_s...]
where the time goes in v2:
time: 24.5 us; the launch traced here: 24.3 us
  Pallas kernels  22.8 us (93%)
  local copies, waits for them, and re-layouts  0.86 us (4%)
  between operations  0.66 us (3%)
    pallas_call x1, Pallas kernels, local(): pl.pallas_call(functools.partial(kernel, sections, experts, chunk), out_s...  22.8 us
    unnamed x1, local copies, waits for them, and re-layouts  0.86 us

profile of v2, /device:TPU:0, one launch (start us, length us, event | category | flops | bytes accessed | tf_op | source)
XLA Modules:
  0.0 24.3 jit_solution(10725948804585562753)
XLA Ops:
  0.7 22.8 %shard_map.64 = bf16[256,1408]{1,0:T(8,128)(2,1)S(1)} custom-call(bf16[256,1408]{1,0:T(8,128)(2,1)} %bitcast.8, bf16[1408]{0:T(1024)(128)(2,1)} %gain_ref.1, bf16[16,1408]{1,0:T(8,128)(2,1)} %bitcast.9, f32[1]{0:T(128)S(6)} %copy.9.scale_ref, bf16[2560,1408]{1,0:T(8,128)(2,1)} %bitcast.6, bf16[2560,1408]{1,0:T(8,128)(2,1)} %bitcast.7), custom_call_target="tpu_custom_call" | custom-call | tf_op jit(solution)/shard_map/pallas_call | solution.py:198
  23.4 0.9 %copy.8 = bf16[1,256,1408]{2,1,0:T(8,128)(2,1)} copy(bf16[1,256,1408]{2,1,0:T(8,128)(2,1)S(1)} %bitcast.5) | data formatting | bytes 1441792

commit v3 on v2

--- a/solution.py
+++ b/solution.py
@@ -189,7 +189,7 @@
         slots = slot_map.shape[1]
         assert count == 1 and held == 1 and slots == experts
         half = -(-width // 256) * 128
-        chunk = split_of(hidden_units, 512, 128)
+        chunk = split_of(hidden_units, 1280, 128)
         chunks = hidden_units // chunk
         bf16 = jnp.bfloat16
         hbm = pl.BlockSpec(memory_space=pl.ANY)

time: 24.5 us -> 23.9 us (0.976)
  Pallas kernels: 22.8 us -> 22.1 us
    pallas_call x1, Pallas kernels: 22.8 us -> 22.1 us  [local(): pl.pallas_call(functools.partial(kernel, sections, experts, chunk), out_s...]
where the time goes in v3:
time: 23.9 us; the launch traced here: 23.7 us
  Pallas kernels  22.1 us (92%)
  local copies, waits for them, and re-layouts  0.86 us (4%)
  between operations  0.66 us (3%)
    pallas_call x1, Pallas kernels, local(): pl.pallas_call(functools.partial(kernel, sections, experts, chunk), out_s...  22.1 us
    unnamed x1, local copies, waits for them, and re-layouts  0.86 us

profile of v3, /device:TPU:0, one launch (start us, length us, event | category | flops | bytes accessed | tf_op | source)
XLA Modules:
  0.0 23.7 jit_solution(17597890237698460756)
XLA Ops:
  0.7 22.1 %shard_map.64 = bf16[256,1408]{1,0:T(8,128)(2,1)S(1)} custom-call(bf16[256,1408]{1,0:T(8,128)(2,1)} %bitcast.8, bf16[1408]{0:T(1024)(128)(2,1)} %gain_ref.1, bf16[16,1408]{1,0:T(8,128)(2,1)} %bitcast.9, f32[1]{0:T(128)S(6)} %copy.9.scale_ref, bf16[2560,1408]{1,0:T(8,128)(2,1)} %bitcast.6, bf16[2560,1408]{1,0:T(8,128)(2,1)} %bitcast.7), custom_call_target="tpu_custom_call" | custom-call | tf_op jit(solution)/shard_map/pallas_call | solution.py:198
  22.8 0.9 %copy.8 = bf16[1,256,1408]{2,1,0:T(8,128)(2,1)} copy(bf16[1,256,1408]{2,1,0:T(8,128)(2,1)S(1)} %bitcast.5) | data formatting | bytes 1441792
